TPU v7x, 64 devices: a 2x2x8 block of a 4x4x8 slice. The times are simulated.
64 devices in a mesh: rep: 4 (over x, y), dp: 16 (over z, core).
Axes of the slice: x: 2, y: 2, z: 8, core: 2. Of those that a mesh axis runs over, the one named last changes fastest.
The devices are a block of a 4x4x8 slice.
Arguments:
- a: bfloat16 [64, 4, 2048, 896], P(('rep', 'dp')), parts along dimension 0
- g: bfloat16 [64, 4, 2048, 4736], P(('rep', 'dp')), parts along dimension 0
Outputs:
- output: bfloat16 [16, 896, 4736], P('rep'), parts along dimension 0
There are 4 independent parts. A program takes and returns all parts, laid end to end along the dimension named above; each array names one.
All inputs are finite; a program needn't handle non-finite values.
Results may differ from a plain program's by a relative error of at most 0.012.
Values are sent between devices in bfloat16 or wider.
A program may use at most 768 MiB of HBM per device.

v0:
```python
import functools

import jax
import jax.numpy as jnp
from jax import lax
from jax.experimental import pallas as pl
from jax.experimental.pallas import tpu as pltpu
from jax.sharding import PartitionSpec as P

MESH = pl.DeviceIdType.MESH
CORES = 2
TILE = 512
KBLOCK = 256
STAGES = 4
WRITES = 16


def kernel(chips, a_ref, g_ref, x_ref, stage, at, gp, go, acc, pbuf, pin,
           stage_sem, gp_sem, go_sem, psend, precv, osend, rrecv, gsend, dsend, grecv, drecv, clear):
    _, mats, tokens, depth = a_ref.shape
    width = g_ref.shape[3]
    rows = at.shape[1]
    per_mat = depth // rows
    full = width // TILE
    widths = [TILE] * full + ([width - full * TILE] if width % TILE else [])
    tiles = len(widths)
    total = chips * tiles

    dp = lax.axis_index("dp")
    z, c = dp // CORES, dp % CORES
    d = 1 - 2 * c
    nxt = lax.rem(z + d + chips, chips) * CORES + c
    prv = lax.rem(z - d + chips, chips) * CORES + c
    par = z * CORES + 1 - c

    def mine(s):
        return lax.rem(z - d * (s + 1) + 2 * chips, chips)

    def theirs(s):
        return lax.rem(z + d * (s + 1) + 2 * chips, chips)

    def columns(j, w):
        return pl.ds(j * TILE if isinstance(j, int) else pl.multiple_of(j * TILE, TILE), w)

    def g_copy(buf, sem, mat, j, w, slot):
        return pltpu.make_async_copy(g_ref.at[0, mat, :, columns(j, w)], buf.at[slot, :, pl.ds(0, w)], sem.at[slot])

    def g_start(buf, sem, chunk, t):
        s, j = t // tiles, t % tiles
        mat = chunk(s) * CORES // per_mat

        @pl.when((t < total) & (j < full))
        def _():
            g_copy(buf, sem, mat, j, TILE, t % 2).start()

        if tiles > full:
            @pl.when((t < total) & (j == full))
            def _():
                g_copy(buf, sem, mat, full, widths[full], t % 2).start()

    some = tokens // STAGES

    def a_copy(mat, k):
        return pltpu.make_async_copy(
            a_ref.at[0, mat, pl.ds(pl.multiple_of(k * some, some), some)], stage.at[k], stage_sem.at[k])

    def transpose(i):
        @pl.loop(0, STAGES)
        def _(k):
            a_copy(order[i], k).wait()
            for b in range(some // KBLOCK):
                span = pl.ds(pl.multiple_of(k * some + b * KBLOCK, KBLOCK), KBLOCK)
                block = stage[k, b * KBLOCK:(b + 1) * KBLOCK, :].T
                for r in range(per_mat):
                    at[order[i] * per_mat + r, :, span] = block[r * rows:(r + 1) * rows]
            if i + 1 < mats:
                a_copy(order[i + 1], k).start()

    def to_partner(t, j, w):
        return pltpu.make_async_remote_copy(
            pbuf.at[j, :, pl.ds(0, w)], pin.at[t % 4, :, pl.ds(0, w)], psend.at[j], precv.at[t % 4],
            device_id={"dp": par}, device_id_type=MESH)

    def place(chunk, core, j, w):
        return x_ref.at[pl.ds(pl.multiple_of((chunk * CORES + core) * rows, rows), rows), columns(j, w)]

    def to_next(s, j, w):
        here = place(mine(s), c, j, w)
        return pltpu.make_async_remote_copy(
            here, here, osend.at[j], rrecv.at[s, j], device_id={"dp": nxt}, device_id_type=MESH)

    def gather(s, j, w):
        here = place(lax.rem(z - d * s + 2 * chips, chips), c, j, w)
        return pltpu.make_async_remote_copy(
            here, here, gsend, grecv.at[s, j], device_id={"dp": nxt}, device_id_type=MESH)

    def share(s, j, w):
        here = place(lax.rem(z - d * s + 2 * chips, chips), c, j, w)
        return pltpu.make_async_remote_copy(
            here, here, dsend, drecv.at[s, j], device_id={"dp": par}, device_id_type=MESH)

    def partner_term(s, j, w):
        t = s * tiles + j
        slot = t % 2
        chunk = theirs(s)
        g_copy(gp, gp_sem, chunk * CORES // per_mat, j, w, slot).wait()

        @pl.when(s > 0)
        def _():
            to_partner(t, j, w).wait_send()

        pbuf[j, :, :w] = jnp.dot(
            at[chunk * CORES + 1 - c], gp[slot, :, :w], preferred_element_type=jnp.float32).astype(jnp.bfloat16)
        to_partner(t, j, w).start()

    def own_term(s, j, w):
        t = s * tiles + j
        slot = t % 2
        chunk = mine(s)
        g_copy(go, go_sem, chunk * CORES // per_mat, j, w, slot).wait()
        acc[:, :w] = jnp.dot(at[chunk * CORES + c], go[slot, :, :w], preferred_element_type=jnp.float32)
        to_partner(t, j, w).wait_recv()

        here = place(chunk, c, j, w)

        @pl.when(s == 0)
        def _():
            here[...] = (acc[:, :w] + pin[t % 4, :, :w].astype(jnp.float32)).astype(jnp.bfloat16)

        @pl.when(s > 0)
        def _():
            to_next(s - 1, j, w).wait()
            here[...] = (
                acc[:, :w] + pin[t % 4, :, :w].astype(jnp.float32) + here[...].astype(jnp.float32)
            ).astype(jnp.bfloat16)

        @pl.when(s < chips - 1)
        def _():
            to_next(s, j, w).start()

        @pl.when(s == chips - 1)
        def _():
            gather(0, j, w).start()
            share(0, j, w).start()

    barrier = pltpu.get_barrier_semaphore()
    for who in (nxt, prv, par):
        pl.semaphore_signal(barrier, inc=1, device_id={"dp": who}, device_id_type=MESH)

    order = [theirs(0) * CORES // per_mat, mine(0) * CORES // per_mat]
    early = lax.rem((z + chips - 1) // CORES, mats)
    order += [lax.rem(early + i, mats) for i in range(2, mats)]
    for k in range(STAGES):
        a_copy(order[0], k).start()
    g_start(gp, gp_sem, theirs, 0)
    g_start(go, go_sem, mine, 0)
    g_start(gp, gp_sem, theirs, 1)
    transpose(0)
    pl.semaphore_wait(barrier, 3)
    partner_term(0, 0, widths[0])
    transpose(1)

    def step(s, j, w, w_after):
        t = s * tiles + j
        g_start(gp, gp_sem, theirs, t + 2)
        g_start(go, go_sem, mine, t + 1)
        if w_after is None:
            @pl.when(s < chips - 1)
            def _():
                partner_term(s + 1, 0, widths[0])
        else:
            partner_term(s, j + 1, w_after)
        own_term(s, j, w)

    @pl.loop(0, chips)
    def _(s):
        @pl.loop(0, full - 1)
        def _(j):
            step(s, j, TILE, TILE)
            for i in range(2, mats):
                @pl.when((s == 0) & (j == 2 * i - 2))
                def _():
                    transpose(i)

        for j in range(full - 1, tiles):
            step(s, j, widths[j], widths[j + 1] if j + 1 < tiles else None)

    pl.semaphore_signal(clear, inc=1, device_id={"dp": prv}, device_id_type=MESH)
    for j, w in enumerate(widths):
        to_partner((chips - 1) * tiles + j, j, w).wait_send()

    @pl.loop(1, chips)
    def _(s):
        @pl.when(s == chips - 3)
        def _():
            pl.semaphore_wait(clear, 1)

        for j, w in enumerate(widths):
            gather(s - 1, j, w).wait_recv()

            @pl.when(s < chips - 1)
            def _():
                gather(s, j, w).start()

            share(s, j, w).start()

    @pl.loop(0, chips)
    def _(s):
        for j, w in enumerate(widths):
            share(s, j, w).wait_recv()

    def all_bytes(chunks, sem):
        part = x_ref.at[pl.ds(0, chunks * rows)]
        pltpu.make_async_copy(part, part, sem).wait()

    all_bytes(chips - 1, gsend)
    all_bytes(chips, dsend)


def writer(x_ref, o_ref, sem):
    part = x_ref.shape[0] // WRITES
    copies = [
        pltpu.make_async_copy(x_ref.at[pl.ds(i * part, part)], o_ref.at[pl.ds(i * part, part)], sem.at[i])
        for i in range(WRITES)
    ]
    for copy in copies:
        copy.start()
    for copy in copies:
        copy.wait()


def solution(mesh):
    members = mesh.shape["dp"]
    chips = members // CORES

    def body(a, g):
        _, mats, tokens, depth = a.shape
        width = g.shape[3]
        rows = mats * depth // members
        tiles = pl.cdiv(width, TILE)
        bf16, f32, dma = jnp.bfloat16, jnp.float32, pltpu.SemaphoreType.DMA
        sums = pl.pallas_call(
            functools.partial(kernel, chips),
            out_shape=pltpu.VMEM((mats * depth, width), bf16),
            in_specs=[pl.BlockSpec(memory_space=pl.ANY)] * 2,
            out_specs=pl.BlockSpec(memory_space=pltpu.VMEM),
            scratch_shapes=[
                pltpu.VMEM((STAGES, tokens // STAGES, depth), bf16),
                pltpu.VMEM((members, rows, tokens), bf16),
                pltpu.VMEM((2, tokens, TILE), bf16),
                pltpu.VMEM((2, tokens, TILE), bf16),
                pltpu.VMEM((rows, TILE), f32),
                pltpu.VMEM((tiles, rows, TILE), bf16),
                pltpu.VMEM((4, rows, TILE), bf16),
                dma((STAGES,)), dma((2,)), dma((2,)),
                dma((tiles,)), dma((4,)), dma((tiles,)), dma((chips - 1, tiles)),
                dma, dma,
                dma((chips - 1, tiles)), dma((chips, tiles)),
                pltpu.SemaphoreType.REGULAR,
            ],
            compiler_params=pltpu.CompilerParams(
                collective_id=0, has_side_effects=True, vmem_limit_bytes=30 * 2**20),
        )(a, g)
        out = pl.pallas_call(
            writer,
            out_shape=jax.ShapeDtypeStruct((mats * depth, width), bf16),
            in_specs=[pl.BlockSpec(memory_space=pltpu.VMEM)],
            out_specs=pl.BlockSpec(memory_space=pl.ANY),
            scratch_shapes=[dma((WRITES,))],
            compiler_params=pltpu.CompilerParams(vmem_limit_bytes=2**20),
        )(sums)
        return out.reshape(mats, depth, width)

    part = P(("rep", "dp"))
    return jax.shard_map(body, mesh=mesh, in_specs=(part, part), out_specs=P("rep"), check_vma=False)
```

profile of v0, /device:TPU:21, one launch (start us, length us, event | category | flops | bytes accessed | tf_op | source)
XLA Modules:
  0.0 349.7 jit_solution(18397082915660966569)
XLA Ops:
  0.0 338.6 %shard_map.28.x_ref = bf16[3584,4736]{1,0:T(8,128)(2,1)S(1)} custom-call(bf16[1,4,2048,896]{3,2,1,0:T(8,128)(2,1)} %a_ref.1, bf16[1,4,2048,4736]{3,2,1,0:T(8,128)(2,1)} %g_ref.1), custom_call_target="tpu_custom_call" | custom-call | tf_op jit(solution)/shard_map/pallas_call | solution.py:242
  338.6 11.2 %shard_map.29 = bf16[3584,4736]{1,0:T(8,128)(2,1)} custom-call(bf16[3584,4736]{1,0:T(8,128)(2,1)S(1)} %shard_map.28.x_ref), custom_call_target="tpu_custom_call" | custom-call | tf_op jit(solution)/shard_map/pallas_call | solution.py:264
where the time goes:
time: 350 us
  Pallas kernels  350 us (100%)
    pallas_call x1, Pallas kernels, body(): pl.pallas_call(functools.partial(kernel, chips), out_shape=pltpu.VMEM((ma...  339 us
    pallas_call x1, Pallas kernels, body(): pl.pallas_call(writer, out_shape=jax.ShapeDtypeStruct((mats * depth, widt...  11.2 us

commit v1 on v0

--- a/solution.py
+++ b/solution.py
@@ -12,11 +12,12 @@
 TILE = 512
 KBLOCK = 256
 STAGES = 4
+LANES = 128
 WRITES = 16
 
 
 def kernel(chips, a_ref, g_ref, x_ref, stage, at, gp, go, acc, pbuf, pin,
-           stage_sem, gp_sem, go_sem, psend, precv, osend, rrecv, gsend, dsend, grecv, drecv, clear):
+           stage_sem, early_sem, gp_sem, go_sem, psend, precv, osend, rrecv, gsend, dsend, grecv, drecv, clear):
     _, mats, tokens, depth = a_ref.shape
     width = g_ref.shape[3]
     rows = at.shape[1]
@@ -76,6 +77,33 @@
             if i + 1 < mats:
                 a_copy(order[i + 1], k).start()
 
+    spans = [r * rows // LANES * LANES for r in range(per_mat)]
+    cover = max(pl.cdiv((r + 1) * rows - spans[r], LANES) * LANES for r in range(per_mat))
+    spans = [min(first, depth - cover) for first in spans]
+
+    def early_copy(block, r, n, k):
+        return pltpu.make_async_copy(
+            a_ref.at[0, block // per_mat, pl.ds(k * some, some), pl.ds(spans[r], cover)],
+            stage.at[k, :, pl.ds(n * cover, cover)], early_sem.at[n, k])
+
+    def early_start(block, n):
+        for r in range(per_mat):
+            @pl.when(block % per_mat == r)
+            def _():
+                for k in range(STAGES):
+                    early_copy(block, r, n, k).start()
+
+    def early_transpose(block, n):
+        for r in range(per_mat):
+            @pl.when(block % per_mat == r)
+            def _():
+                for k in range(STAGES):
+                    early_copy(block, r, n, k).wait()
+                    for b in range(some // KBLOCK):
+                        part = stage[k, b * KBLOCK:(b + 1) * KBLOCK, n * cover:(n + 1) * cover].T
+                        at[block, :, k * some + b * KBLOCK:k * some + (b + 1) * KBLOCK] = (
+                            part[r * rows - spans[r]:(r + 1) * rows - spans[r]])
+
     def to_partner(t, j, w):
         return pltpu.make_async_remote_copy(
             pbuf.at[j, :, pl.ds(0, w)], pin.at[t % 4, :, pl.ds(0, w)], psend.at[j], precv.at[t % 4],
@@ -147,18 +175,22 @@
     for who in (nxt, prv, par):
         pl.semaphore_signal(barrier, inc=1, device_id={"dp": who}, device_id_type=MESH)
 
-    order = [theirs(0) * CORES // per_mat, mine(0) * CORES // per_mat]
-    early = lax.rem((z + chips - 1) // CORES, mats)
-    order += [lax.rem(early + i, mats) for i in range(2, mats)]
+    block_p, block_o = theirs(0) * CORES + 1 - c, mine(0) * CORES + c
+    early_start(block_p, 0)
+    g_start(gp, gp_sem, theirs, 0)
+    early_start(block_o, 1)
+    g_start(go, go_sem, mine, 0)
+    g_start(gp, gp_sem, theirs, 1)
+    early_transpose(block_p, 0)
+    pl.semaphore_wait(barrier, 3)
+    partner_term(0, 0, widths[0])
+    early_transpose(block_o, 1)
+
+    base = z * CORES // per_mat
+    order = [lax.rem(base + ahead, mats) for ahead in (mats - 1, 1, 2, 0)]
+    times = [(0, 1), (0, 4), (1, 1), (2, 1)]
     for k in range(STAGES):
         a_copy(order[0], k).start()
-    g_start(gp, gp_sem, theirs, 0)
-    g_start(go, go_sem, mine, 0)
-    g_start(gp, gp_sem, theirs, 1)
-    transpose(0)
-    pl.semaphore_wait(barrier, 3)
-    partner_term(0, 0, widths[0])
-    transpose(1)
 
     def step(s, j, w, w_after):
         t = s * tiles + j
@@ -177,8 +209,8 @@
         @pl.loop(0, full - 1)
         def _(j):
             step(s, j, TILE, TILE)
-            for i in range(2, mats):
-                @pl.when((s == 0) & (j == 2 * i - 2))
+            for i, (when_s, when_j) in enumerate(times):
+                @pl.when((s == when_s) & (j == when_j))
                 def _():
                     transpose(i)
 
@@ -203,11 +235,10 @@
                 gather(s, j, w).start()
 
             share(s, j, w).start()
-
-    @pl.loop(0, chips)
-    def _(s):
-        for j, w in enumerate(widths):
-            share(s, j, w).wait_recv()
+            share(s - 1, j, w).wait_recv()
+
+    for j, w in enumerate(widths):
+        share(chips - 1, j, w).wait_recv()
 
     def all_bytes(chunks, sem):
         part = x_ref.at[pl.ds(0, chunks * rows)]
@@ -252,7 +283,7 @@
                 pltpu.VMEM((rows, TILE), f32),
                 pltpu.VMEM((tiles, rows, TILE), bf16),
                 pltpu.VMEM((4, rows, TILE), bf16),
-                dma((STAGES,)), dma((2,)), dma((2,)),
+                dma((STAGES,)), dma((2, STAGES)), dma((2,)), dma((2,)),
                 dma((tiles,)), dma((4,)), dma((tiles,)), dma((chips - 1, tiles)),
                 dma, dma,
                 dma((chips - 1, tiles)), dma((chips, tiles)),

time: 350 us -> 349 us (level)
  no operation moved by 1% of the time
where the time goes in v1:
time: 349 us; the launch traced here: 348 us
  Pallas kernels  348 us (100%)
    pallas_call x1, Pallas kernels, body(): pl.pallas_call(functools.partial(kernel, chips), out_shape=pltpu.VMEM((ma...  337 us
    pallas_call x1, Pallas kernels, body(): pl.pallas_call(writer, out_shape=jax.ShapeDtypeStruct((mats * depth, widt...  11.2 us

profile of v1, /device:TPU:21, one launch (start us, length us, event | category | flops | bytes accessed | tf_op | source)
XLA Modules:
  0.0 348.4 jit_solution(16373156078152620123)
XLA Ops:
  0.0 337.2 %shard_map.28.x_ref = bf16[3584,4736]{1,0:T(8,128)(2,1)S(1)} custom-call(bf16[1,4,2048,896]{3,2,1,0:T(8,128)(2,1)} %a_ref.1, bf16[1,4,2048,4736]{3,2,1,0:T(8,128)(2,1)} %g_ref.1), custom_call_target="tpu_custom_call" | custom-call | tf_op jit(solution)/shard_map/pallas_call | solution.py:273
  337.2 11.2 %shard_map.29 = bf16[3584,4736]{1,0:T(8,128)(2,1)} custom-call(bf16[3584,4736]{1,0:T(8,128)(2,1)S(1)} %shard_map.28.x_ref), custom_call_target="tpu_custom_call" | custom-call | tf_op jit(solution)/shard_map/pallas_call | solution.py:295

commit v2 on v1

--- a/solution.py
+++ b/solution.py
@@ -33,6 +33,7 @@
     nxt = lax.rem(z + d + chips, chips) * CORES + c
     prv = lax.rem(z - d + chips, chips) * CORES + c
     par = z * CORES + 1 - c
+    beyond = lax.rem(z + d + chips, chips) * CORES + 1 - c
 
     def mine(s):
         return lax.rem(z - d * (s + 1) + 2 * chips, chips)
@@ -93,12 +94,14 @@
                 for k in range(STAGES):
                     early_copy(block, r, n, k).start()
 
-    def early_transpose(block, n):
+    def early_transpose(block, n, meanwhile=lambda: None):
         for r in range(per_mat):
             @pl.when(block % per_mat == r)
             def _():
                 for k in range(STAGES):
                     early_copy(block, r, n, k).wait()
+                    if k == 0:
+                        meanwhile()
                     for b in range(some // KBLOCK):
                         part = stage[k, b * KBLOCK:(b + 1) * KBLOCK, n * cover:(n + 1) * cover].T
                         at[block, :, k * some + b * KBLOCK:k * some + (b + 1) * KBLOCK] = (
@@ -126,6 +129,11 @@
         here = place(lax.rem(z - d * s + 2 * chips, chips), c, j, w)
         return pltpu.make_async_remote_copy(
             here, here, dsend, drecv.at[s, j], device_id={"dp": par}, device_id_type=MESH)
+
+    def last_share(w):
+        here = place(lax.rem(z - d * (chips - 2) + 2 * chips, chips), c, tiles - 1, w)
+        return pltpu.make_async_remote_copy(
+            here, here, dsend, drecv.at[chips - 1, tiles - 1], device_id={"dp": beyond}, device_id_type=MESH)
 
     def partner_term(s, j, w):
         t = s * tiles + j
@@ -172,17 +180,16 @@
             share(0, j, w).start()
 
     barrier = pltpu.get_barrier_semaphore()
-    for who in (nxt, prv, par):
+    for who in (nxt, prv, par, beyond):
         pl.semaphore_signal(barrier, inc=1, device_id={"dp": who}, device_id_type=MESH)
 
     block_p, block_o = theirs(0) * CORES + 1 - c, mine(0) * CORES + c
     early_start(block_p, 0)
     g_start(gp, gp_sem, theirs, 0)
     early_start(block_o, 1)
-    g_start(go, go_sem, mine, 0)
+    early_transpose(block_p, 0, lambda: g_start(go, go_sem, mine, 0))
     g_start(gp, gp_sem, theirs, 1)
-    early_transpose(block_p, 0)
-    pl.semaphore_wait(barrier, 3)
+    pl.semaphore_wait(barrier, 4)
     partner_term(0, 0, widths[0])
     early_transpose(block_o, 1)
 
@@ -191,6 +198,11 @@
     times = [(0, 1), (0, 4), (1, 1), (2, 1)]
     for k in range(STAGES):
         a_copy(order[0], k).start()
+
+    g_start(gp, gp_sem, theirs, 2)
+    g_start(go, go_sem, mine, 1)
+    own_term(0, 0, widths[0])
+    partner_term(0, 1, widths[1])
 
     def step(s, j, w, w_after):
         t = s * tiles + j
@@ -208,7 +220,10 @@
     def _(s):
         @pl.loop(0, full - 1)
         def _(j):
-            step(s, j, TILE, TILE)
+            @pl.when(s + j > 0)
+            def _():
+                step(s, j, TILE, TILE)
+
             for i, (when_s, when_j) in enumerate(times):
                 @pl.when((s == when_s) & (j == when_j))
                 def _():
@@ -234,7 +249,16 @@
             def _():
                 gather(s, j, w).start()
 
-            share(s, j, w).start()
+            if j == tiles - 1:
+                @pl.when(s == chips - 2)
+                def _():
+                    last_share(w).start()
+
+                @pl.when(s < chips - 1)
+                def _():
+                    share(s, j, w).start()
+            else:
+                share(s, j, w).start()
             share(s - 1, j, w).wait_recv()
 
     for j, w in enumerate(widths):

time: 349 us -> 348 us (level)
  no operation moved by 1% of the time
where the time goes in v2:
time: 348 us
  Pallas kernels  348 us (100%)
    pallas_call x1, Pallas kernels, body(): pl.pallas_call(functools.partial(kernel, chips), out_shape=pltpu.VMEM((ma...  337 us
    pallas_call x1, Pallas kernels, body(): pl.pallas_call(writer, out_shape=jax.ShapeDtypeStruct((mats * depth, widt...  11.2 us

profile of v2, /device:TPU:21, one launch (start us, length us, event | category | flops | bytes accessed | tf_op | source)
XLA Modules:
  0.0 348.0 jit_solution(9004072398537616021)
XLA Ops:
  0.0 336.8 %shard_map.28.x_ref = bf16[3584,4736]{1,0:T(8,128)(2,1)S(1)} custom-call(bf16[1,4,2048,896]{3,2,1,0:T(8,128)(2,1)} %a_ref.1, bf16[1,4,2048,4736]{3,2,1,0:T(8,128)(2,1)} %g_ref.1), custom_call_target="tpu_custom_call" | custom-call | tf_op jit(solution)/shard_map/pallas_call | solution.py:297
  336.8 11.2 %shard_map.29 = bf16[3584,4736]{1,0:T(8,128)(2,1)} custom-call(bf16[3584,4736]{1,0:T(8,128)(2,1)S(1)} %shard_map.28.x_ref), custom_call_target="tpu_custom_call" | custom-call | tf_op jit(solution)/shard_map/pallas_call | solution.py:319

commit v3 on v2

--- a/solution.py
+++ b/solution.py
@@ -195,9 +195,7 @@
 
     base = z * CORES // per_mat
     order = [lax.rem(base + ahead, mats) for ahead in (mats - 1, 1, 2, 0)]
-    times = [(0, 1), (0, 4), (1, 1), (2, 1)]
-    for k in range(STAGES):
-        a_copy(order[0], k).start()
+    times = [(0, 5), (0, 7), (1, 5), (2, 5)]
 
     g_start(gp, gp_sem, theirs, 2)
     g_start(go, go_sem, mine, 1)
@@ -223,6 +221,11 @@
             @pl.when(s + j > 0)
             def _():
                 step(s, j, TILE, TILE)
+
+            @pl.when((s == 0) & (j == times[0][1] - 2))
+            def _():
+                for k in range(STAGES):
+                    a_copy(order[0], k).start()
 
             for i, (when_s, when_j) in enumerate(times):
                 @pl.when((s == when_s) & (j == when_j))

time: 348 us -> 347 us (level)
  no operation moved by 1% of the time
where the time goes in v3:
time: 347 us
  Pallas kernels  347 us (100%)
    pallas_call x1, Pallas kernels, body(): pl.pallas_call(functools.partial(kernel, chips), out_shape=pltpu.VMEM((ma...  336 us
    pallas_call x1, Pallas kernels, body(): pl.pallas_call(writer, out_shape=jax.ShapeDtypeStruct((mats * depth, widt...  11.2 us

profile of v3, /device:TPU:21, one launch (start us, length us, event | category | flops | bytes accessed | tf_op | source)
XLA Modules:
  0.0 346.9 jit_solution(12484332933239878234)
XLA Ops:
  0.0 335.7 %shard_map.28.x_ref = bf16[3584,4736]{1,0:T(8,128)(2,1)S(1)} custom-call(bf16[1,4,2048,896]{3,2,1,0:T(8,128)(2,1)} %a_ref.1, bf16[1,4,2048,4736]{3,2,1,0:T(8,128)(2,1)} %g_ref.1), custom_call_target="tpu_custom_call" | custom-call | tf_op jit(solution)/shard_map/pallas_call | solution.py:300
  335.7 11.2 %shard_map.29 = bf16[3584,4736]{1,0:T(8,128)(2,1)} custom-call(bf16[3584,4736]{1,0:T(8,128)(2,1)S(1)} %shard_map.28.x_ref), custom_call_target="tpu_custom_call" | custom-call | tf_op jit(solution)/shard_map/pallas_call | solution.py:322
